TPU v7x, 256 devices: a whole 4x4x8 slice. The times are simulated.
256 devices in a mesh: expert: 16 (over x, y), tensor: 8 (over z), replica: 2 (over core).
Axes of the slice: x: 4, y: 4, z: 8, core: 2. Of those that a mesh axis runs over, the one named last changes fastest.
Arguments:
- trained: float32 [16, 7168, 2048], P('replica', 'tensor', 'expert'), may hold values from -3080 to 3080
- snapshot: bfloat16 [16, 7168, 2048], P('replica', 'tensor', 'expert'), may hold values from -3072 to 3072
- changed: int32 [16, 56, 16], P('replica', 'tensor', 'expert'), may hold values from 0 to 1, as said below
- placement: int32 [16], replicated, may hold values from 0 to 15, each once
Outputs:
- rotated_update: bfloat16 [16, 7168, 2048], P('expert', None, 'tensor')
Inputs may be any that keep to these rules, and one draw needn't show every extreme that they name: `placement`: each of the 16 experts appears exactly once. `changed`: in each aligned block of 7 block rows by 1 block columns of one expert, at most 4 entries are 1; for every expert some such block has exactly 4.
All inputs are finite; a program needn't handle non-finite values.
Results may differ from a plain program's by a relative error of at most 0.001.
Values may be sent and summed in bfloat16 or wider, within the bound.
A program may use at most 64 MiB of HBM per device.

v0:
```python
import math
import jax
import jax.numpy as jnp
from jax import lax
from jax.sharding import PartitionSpec as P

BLK = 128


def hadamard():
    positions = jnp.arange(BLK, dtype=jnp.int32)
    parity = jnp.zeros((BLK, BLK), jnp.int32)
    for bit_level in range(BLK.bit_length() - 1):
        parity = parity + (positions[:, None] >> bit_level & 1) * (
            positions[None, :] >> bit_level & 1
        )
    return (1 - 2 * (parity % 2)).astype(jnp.float32) / math.sqrt(BLK)


def body(trained, snapshot, changed, placement):
    hadamard_table = hadamard()
    local_experts, local_rows, local_cols = trained.shape
    copies = lax.axis_size("replica")
    tensor_count = lax.axis_size("tensor")
    expert_count = lax.axis_size("expert")
    members = expert_count // tensor_count
    slot_total = placement.shape[0]
    owner_slots = slot_total // expert_count
    block_rows = local_rows // BLK
    block_cols = local_cols // BLK
    part_rows = BLK // copies
    block_count = block_rows * block_cols
    capacity = (4 * block_count + 3) // 7
    block_flags = changed.reshape(local_experts, block_count)
    position = jnp.arange(block_count, dtype=jnp.int32)
    ranking = jnp.where(block_flags == 1, position[None, :], block_count + position[None, :])
    picked = jnp.argsort(ranking, axis=1)[:, :capacity]
    used_slots = jnp.take_along_axis(block_flags, picked, axis=1)
    expert_ids = jnp.arange(local_experts, dtype=jnp.int32)[:, None]
    row_ids = picked // block_cols
    col_ids = picked % block_cols
    new_tiles = trained.reshape(local_experts, block_rows, BLK, block_cols, BLK)[
        expert_ids, row_ids, :, col_ids, :
    ]
    old_tiles = snapshot.reshape(local_experts, block_rows, BLK, block_cols, BLK)[
        expert_ids, row_ids, :, col_ids, :
    ]
    delta_tiles = jnp.where(
        used_slots[:, :, None, None] == 1, new_tiles - old_tiles.astype(jnp.float32), 0.0
    )
    coded_tiles = jnp.einsum(
        "ij,pmjk->pmik", hadamard_table, delta_tiles, precision=lax.Precision.HIGHEST
    ).astype(jnp.bfloat16)
    coded_tiles = coded_tiles.reshape(local_experts, capacity, copies, part_rows, BLK)
    spots_pair = jnp.broadcast_to(picked[:, :, None], (local_experts, capacity, copies))
    tiles_all, spots_all = (
        lax.all_to_all(coded_tiles, "replica", split_axis=2, concat_axis=0, tiled=True),
        lax.all_to_all(spots_pair, "replica", split_axis=2, concat_axis=0, tiled=True),
    )
    chosen = jnp.take(tiles_all, placement, axis=0).reshape(
        slot_total, 1, 1, capacity, part_rows, BLK
    )
    chosen_spots = jnp.take(spots_all, placement, axis=0).reshape(slot_total, 1, 1, capacity)
    tiles_in, spot_numbers = (
        lax.all_to_all(
            lax.all_to_all(chosen, "expert", split_axis=0, concat_axis=2, tiled=True),
            "tensor",
            split_axis=2,
            concat_axis=1,
            tiled=True,
        ),
        lax.all_to_all(
            lax.all_to_all(chosen_spots, "expert", split_axis=0, concat_axis=2, tiled=True),
            "tensor",
            split_axis=2,
            concat_axis=1,
            tiled=True,
        ),
    )
    source_count = tiles_in.shape[1]
    one_hot = (spot_numbers[..., None] == position).astype(jnp.bfloat16)
    placed = jnp.einsum(
        "osnmg,osnmab->osngab", one_hot, tiles_in, preferred_element_type=jnp.float32
    ).astype(jnp.bfloat16)
    placed = placed.reshape(
        owner_slots, source_count, members, block_rows, block_cols, part_rows, BLK
    )
    placed = jnp.transpose(placed, (0, 1, 3, 5, 2, 4, 6))
    owner_cols = members * block_cols * BLK
    owned_rows = placed.reshape(owner_slots, source_count, block_rows, 1, part_rows, owner_cols)
    whole_rows = lax.all_gather(owned_rows, "replica", axis=3, tiled=True)
    return whole_rows.reshape(owner_slots, tensor_count * block_rows * BLK, owner_cols)


def solution(mesh):
    in_specs = (
        P("replica", "tensor", "expert"),
        P("replica", "tensor", "expert"),
        P("replica", "tensor", "expert"),
        P(),
    )
    out_specs = P("expert", None, "tensor")
    return jax.shard_map(body, mesh=mesh, in_specs=in_specs, out_specs=out_specs, check_vma=False)
```

profile of v0, /device:TPU:1, one launch (start us, length us, event | category | flops | bytes accessed | tf_op | source)
XLA Modules:
  0.0 145.1 jit_solution(11660733728816668597)
XLA Ops:
  6.5 0.9 iota_select_fusion
  8.7 6.4 %all-to-all-start = ((s32[8,4,2]{0,1,2:T(4,128)}), s32[8,4,2]{0,1,2:T(4,128)S(1)}, u32[]{:S(2)}, u32[]{:S(2)}) async-start(s32[8,4,2]{0,1,2:T(4,128)} %broadcast_in_dim.55), calls=%async_computation | async-start | bytes 8192 | tf_op jit(solution)/shard_map/all_to_all | solution.py:58
  16.4 0.8 copy.38
  18.3 0.8 gather_fusion.2
  19.1 4.0 %gather_fusion.1 = f32[32,128,128]{2,1,0:T(8,128)} fusion(f32[8,7,128,1,128]{4,2,1,0,3:T(8,128)} %bitcast.67, s32[32]{0:T(128)S(1)} %reshape.261), kind=kCustom, calls=%fused_computation.1 | custom fusion | bytes 4194688 | tf_op jit(solution)/shard_map/gather | solution.py:42
  23.2 1.9 %convert_subtract_fusion = f32[32,128,128]{2,1,0:T(8,128)S(1)} fusion(f32[32,128,128]{2,1,0:T(8,128)} %gather_fusion.1, bf16[32,128,128]{2,1,0:T(8,128)(2,1)S(1)} %gather_fusion.2), kind=kLoop, calls=%fused_computation.5 | loop fusion | flops 1048576 | bytes 5242880 | tf_op jit(solution)/shard_map/sub | solution.py:49
  25.0 2.3 %fusion.2 = bf16[8,4,128,128]{2,3,1,0:T(8,128)(2,1)S(1)} fusion(f32[8,4,128,128]{3,2,1,0:T(8,128)S(1)} %bitcast.61, pred[8,4]{1,0:T(8,128)(4,1)S(1)} %copy.48, s32[128]{0:T(128)S(1)} %get-tuple-element.7, s32[128]{0:T(128)S(1)} %get-tuple-element.8, s32[128]{0:T(128)S(1)} %get-tuple-element.9, s32[128]{0:T(128)S(1)} %get-tuple-element.10, ...), kind=kOutput, calls=%fused_computation.9 | convolution fusion | flops 806813696 | bytes 3149344 | tf_op jit(solution)/shard_map/ij,pmjk->pmik/dot_general | solution.py:51
  27.3 1.1 copy.49
  28.4 3.6 %all-to-all-start.3 = ((bf16[8,4,2,64,128]{4,3,1,0,2:T(8,128)(2,1)}), bf16[8,4,2,64,128]{4,3,1,0,2:T(8,128)(2,1)S(1)}, u32[]{:S(2)}, u32[]{:S(2)}) async-start(bf16[8,4,2,64,128]{4,3,1,0,2:T(8,128)(2,1)} %copy.49), calls=%async_computation.3 | async-start | bytes 2097152 | tf_op jit(solution)/shard_map/all_to_all | solution.py:57
  32.7 0.7 copy.43
  33.7 5.1 %all-to-all-start.1 = ((s32[16,1,1,4]{3,2,1,0:T(1,128)}), s32[16,1,1,4]{3,2,1,0:T(1,128)}, u32[]{:S(2)}, u32[]{:S(2)}) async-start(s32[16,1,1,4]{3,2,1,0:T(1,128)} %copy.43), calls=%async_computation.1 | async-start | bytes 16384 | tf_op jit(solution)/shard_map/all_to_all | solution.py:73
  38.9 2.0 %gather_fusion.3 = bf16[16,4,64,128]{3,2,1,0:T(8,128)(2,1)S(1)} fusion(bf16[16,4,64,128]{3,2,1,0:T(8,128)(2,1)} %bitcast.65, s32[1024]{0:T(1024)S(1)} %pad_clamp_fusion), kind=kCustom, calls=%fused_computation.3 | custom fusion | bytes 2097216 | tf_op jit(solution)/shard_map/jit(_take)/gather | solution.py:60
  40.8 1.1 fusion.5
  42.0 3.2 %all-to-all-done.1 = s32[16,1,1,4]{3,2,1,0:T(1,128)} async-done(((s32[16,1,1,4]{3,2,1,0:T(1,128)}), s32[16,1,1,4]{3,2,1,0:T(1,128)}, u32[]{:S(2)}, u32[]{:S(2)}) %all-to-all-start.1) | async-done | bytes 288 | tf_op jit(solution)/shard_map/all_to_all | solution.py:73
  45.2 18.6 %all_to_all.78 = bf16[16,1,1,4,64,128]{5,4,3,2,1,0:T(8,128)(2,1)S(1)} all-to-all(bf16[16,1,1,4,64,128]{5,4,3,2,1,0:T(8,128)(2,1)} %fusion.5), channel_id=1, replica_groups=mesh['expert'=16,'tensor'=8,'replica'=2] {'expert'}, dimensions={0} | all-to-all | bytes 2097152 | tf_op jit(solution)/shard_map/all_to_all | solution.py:66
  63.8 32.6 %all_to_all.79 = bf16[1,1,16,4,64,128]{5,4,3,1,0,2:T(8,128)(2,1)} all-to-all(bf16[1,1,16,4,64,128]{5,4,3,1,0,2:T(8,128)(2,1)S(1)} %bitcast.66), channel_id=1, replica_groups=mesh['expert'=16,'tensor'=8,'replica'=2] {'tensor'}, dimensions={2} | all-to-all | bytes 2097152 | tf_op jit(solution)/shard_map/all_to_all | solution.py:65
  96.3 4.3 %all-to-all-start.2 = ((s32[1,1,16,4]{3,1,0,2:T(1,128)}), s32[1,1,16,4]{3,1,0,2:T(1,128)S(1)}, u32[]{:S(2)}, u32[]{:S(2)}) async-start(s32[1,1,16,4]{3,1,0,2:T(1,128)} %bitcast.31), calls=%async_computation.2 | async-start | bytes 16384 | tf_op jit(solution)/shard_map/all_to_all | solution.py:72
  100.7 2.1 %copy.52 = bf16[1,1,16,4,64,128]{5,3,4,2,1,0:T(4,128)(2,1)S(1)} copy(bf16[1,1,16,4,64,128]{5,4,3,1,0,2:T(8,128)(2,1)} %all_to_all.79) | data formatting | bytes 2097152 | tf_op jit(solution)/shard_map/all_to_all | solution.py:65
  102.8 4.4 %all-to-all-done.2 = s32[1,1,16,4]{3,1,0,2:T(1,128)S(1)} async-done(((s32[1,1,16,4]{3,1,0,2:T(1,128)}), s32[1,1,16,4]{3,1,0,2:T(1,128)S(1)}, u32[]{:S(2)}, u32[]{:S(2)}) %all-to-all-start.2) | async-done | bytes 288 | tf_op jit(solution)/shard_map/all_to_all | solution.py:72
  107.2 1.3 convert_bitcast_fusion
  108.5 3.3 %copy.53 = bf16[1,8,7,64,2,1,128]{6,4,3,2,1,5,0:T(2,128)(2,1)} copy(bf16[1,8,7,64,2,1,128]{6,2,3,4,1,5,0:T(8,128)(2,1)S(1)} %convert_bitcast_fusion) | data formatting | bytes 3670016 | tf_op jit(solution)/shard_map/transpose | solution.py:88
  111.8 5.3 %reshape.227 = bf16[1,8,7,1,64,256]{5,4,2,1,3,0:T(8,128)(2,1)} reshape(bf16[1,8,7,64,2,1,128]{6,4,3,2,1,5,0:T(2,128)(2,1)} %copy.53) | data formatting | bytes 3670016 | tf_op jit(solution)/shard_map/reshape | solution.py:90
  117.1 16.8 %all-gather.2.cloned.1.call-done = bf16[1,8,7,2,64,256]{5,4,2,1,0,3:T(8,128)(2,1)} async-done(((bf16[1,8,7,1,64,256]{5,4,2,1,0,3:T(8,128)(2,1)}), bf16[1,8,7,2,64,256]{5,4,2,1,0,3:T(8,128)(2,1)}) %all-gather.2.cloned.1.call-update) | async-done | bytes 3670032 | tf_op jit(solution)/shard_map/all_gather | solution.py:91
  133.9 4.4 %copy.55 = bf16[1,8,7,2,64,256]{5,4,3,2,1,0:T(8,128)(2,1)} copy(bf16[1,8,7,2,64,256]{5,4,2,1,0,3:T(8,128)(2,1)} %all-gather.2.cloned.1.call-done) | data formatting | bytes 7340032 | tf_op jit(solution)/shard_map/all_gather | solution.py:91
  (32 shorter events, 4.8 us)
Async XLA Ops:
  6.5 11.8 %copy-start = (bf16[8,896,128]{2,1,0:T(8,128)(2,1)S(1)}, bf16[8,896,128]{2,1,0:T(8,128)(2,1)}, u32[]{:S(2)}) copy-start(bf16[8,896,128]{2,1,0:T(8,128)(2,1)} %param.5) | copy-start | bytes 5505028
  8.7 19.7 %all-to-all-start = ((s32[8,4,2]{0,1,2:T(4,128)}), s32[8,4,2]{0,1,2:T(4,128)S(1)}, u32[]{:S(2)}, u32[]{:S(2)}) async-start(s32[8,4,2]{0,1,2:T(4,128)} %broadcast_in_dim.55), calls=%async_computation | async-start | bytes 8192 | tf_op jit(solution)/shard_map/all_to_all | solution.py:58
  28.4 5.3 %all-to-all-start.3 = ((bf16[8,4,2,64,128]{4,3,1,0,2:T(8,128)(2,1)}), bf16[8,4,2,64,128]{4,3,1,0,2:T(8,128)(2,1)S(1)}, u32[]{:S(2)}, u32[]{:S(2)}) async-start(bf16[8,4,2,64,128]{4,3,1,0,2:T(8,128)(2,1)} %copy.49), calls=%async_computation.3 | async-start | bytes 2097152 | tf_op jit(solution)/shard_map/all_to_all | solution.py:57
  33.7 5.1 %copy-start.1 = (bf16[8,4,2,64,128]{4,3,1,0,2:T(8,128)(2,1)}, bf16[8,4,2,64,128]{4,3,1,0,2:T(8,128)(2,1)S(1)}, u32[]{:S(2)}) copy-start(bf16[8,4,2,64,128]{4,3,1,0,2:T(8,128)(2,1)S(1)} %all-to-all-done.3) | copy-start | bytes 3145732
  33.7 11.4 %all-to-all-start.1 = ((s32[16,1,1,4]{3,2,1,0:T(1,128)}), s32[16,1,1,4]{3,2,1,0:T(1,128)}, u32[]{:S(2)}, u32[]{:S(2)}) async-start(s32[16,1,1,4]{3,2,1,0:T(1,128)} %copy.43), calls=%async_computation.1 | async-start | bytes 16384 | tf_op jit(solution)/shard_map/all_to_all | solution.py:73
  96.3 10.8 %all-to-all-start.2 = ((s32[1,1,16,4]{3,1,0,2:T(1,128)}), s32[1,1,16,4]{3,1,0,2:T(1,128)S(1)}, u32[]{:S(2)}, u32[]{:S(2)}) async-start(s32[1,1,16,4]{3,1,0,2:T(1,128)} %bitcast.31), calls=%async_computation.2 | async-start | bytes 16384 | tf_op jit(solution)/shard_map/all_to_all | solution.py:72
  100.6 33.3 %all-gather.2.cloned.1.call-start = ((), (), s32[]{:S(2)}) async-start(), calls=%async_computation.6 | async-start | bytes 5505024 | tf_op jit(solution)/shard_map/all_gather | solution.py:91
Sparse Core Ops, SparseCore 0:
  117.2 16.6 all-gather.1
where the time goes:
time: 146 us; the launch traced here: 145 us
  blocking collectives  51.2 us (35%)
  local copies, waits for them, and re-layouts  26.8 us (18%)
  waiting for transfers between devices  24.8 us (17%)
  starting transfers between devices  19.4 us (13%)
  between operations  13.5 us (9%)
  other arithmetic  5.93 us (4%)
  matrix products  3.58 us (2%)
    all_to_all x1, blocking collectives, body(): lax.all_to_all(lax.all_to_all(chosen, 'expert', split_axis=0, concat_axis...  32.6 us
    all_to_all x1, blocking collectives, body(): lax.all_to_all(chosen, 'expert', split_axis=0, concat_axis=2, tiled=True)  18.6 us
    all_gather x1, waiting for transfers between devices, body(): whole_rows = lax.all_gather(owned_rows, 'replica', axis=3, tiled=True)  16.8 us
    all_to_all x1, starting transfers between devices, body(): lax.all_to_all(spots_pair, 'replica', split_axis=2, concat_axis=0, tiled=...  6.41 us
    reshape x1, local copies, waits for them, and re-layouts, body(): placed.reshape(owner_slots, source_count, block_rows, 1, part_rows, owner...  5.3 us
    all_to_all x1, starting transfers between devices, body(): lax.all_to_all(chosen_spots, 'expert', split_axis=0, concat_axis=2, tiled...  5.1 us
    all_to_all x1, waiting for transfers between devices, body(): lax.all_to_all(lax.all_to_all(chosen_spots, 'expert', split_axis=0, conca...  4.42 us
    all_gather x1, local copies, waits for them, and re-layouts, body(): whole_rows = lax.all_gather(owned_rows, 'replica', axis=3, tiled=True)  4.37 us
  transfers between devices with their start and end apart: 5, of which 4 were waited for; matrix products, arithmetic and copies ran while one was open for 14% of the time, Pallas kernels for 0%

commit v1 on v0

--- a/solution.py
+++ b/solution.py
@@ -3,6 +3,7 @@
 import jax.numpy as jnp
 from jax import lax
 from jax.sharding import PartitionSpec as P
+from jax.lax import all_to_all, axis_size
 
 BLK = 128
 
@@ -88,7 +89,13 @@
     placed = jnp.transpose(placed, (0, 1, 3, 5, 2, 4, 6))
     owner_cols = members * block_cols * BLK
     owned_rows = placed.reshape(owner_slots, source_count, block_rows, 1, part_rows, owner_cols)
-    whole_rows = lax.all_gather(owned_rows, "replica", axis=3, tiled=True)
+
+    def edit_bars(buf):
+        arr_now = axis_size("replica")
+        piece_out = jnp.concatenate([buf] * arr_now, 3)
+        return all_to_all(piece_out, "replica", 3, 3, tiled=True)
+
+    whole_rows = edit_bars(owned_rows)
     return whole_rows.reshape(owner_slots, tensor_count * block_rows * BLK, owner_cols)
 
 

time: 146 us -> 127 us (0.87)
  waiting for transfers between devices: 24.8 us -> 8.17 us
  between operations: 13.5 us -> 0.1 us
  blocking collectives: 51.2 us -> 63.1 us
  other arithmetic: 5.93 us -> 8.31 us
  local copies, waits for them, and re-layouts: 26.8 us -> 24.7 us
    all_gather x1 -> x0, waiting for transfers between devices: 16.8 us -> none  [body(): whole_rows = lax.all_gather(owned_rows, 'replica', axis=3, tiled=True)]
    all_to_all x0 -> x1, blocking collectives: none -> 12.4 us  [edit_bars(): return all_to_all(piece_out, 'replica', 3, 3, tiled=True)]
    all_gather x1 -> x0, local copies, waits for them, and re-layouts: 4.37 us -> none  [body(): whole_rows = lax.all_gather(owned_rows, 'replica', axis=3, tiled=True)]
    concatenate x0 -> x1, other arithmetic: none -> 2.39 us  [edit_bars(): piece_out = jnp.concatenate([buf] * arr_now, 3)]
    all_to_all x0 -> x1, local copies, waits for them, and re-layouts: none -> 2.29 us  [edit_bars(): return all_to_all(piece_out, 'replica', 3, 3, tiled=True)]
  transfers between devices with their start and end apart: 5 -> 4, of which waited for: 4 -> 3; matrix products, arithmetic and copies ran while one was open for 14% -> 16% of each run, Pallas kernels for 0% -> 0%
where the time goes in v1:
time: 127 us
  blocking collectives  63.1 us (50%)
  local copies, waits for them, and re-layouts  24.7 us (19%)
  starting transfers between devices  18.8 us (15%)
  other arithmetic  8.31 us (7%)
  waiting for transfers between devices  8.17 us (6%)
  matrix products  3.58 us (3%)
    all_to_all x1, blocking collectives, body(): lax.all_to_all(lax.all_to_all(chosen, 'expert', split_axis=0, concat_axis...  32.4 us
    all_to_all x1, blocking collectives, body(): lax.all_to_all(chosen, 'expert', split_axis=0, concat_axis=2, tiled=True)  18.3 us
    all_to_all x1, blocking collectives, edit_bars(): return all_to_all(piece_out, 'replica', 3, 3, tiled=True)  12.4 us
    all_to_all x1, starting transfers between devices, body(): lax.all_to_all(spots_pair, 'replica', split_axis=2, concat_axis=0, tiled=...  6.41 us
    reshape x1, local copies, waits for them, and re-layouts, body(): placed.reshape(owner_slots, source_count, block_rows, 1, part_rows, owner...  5.27 us
    all_to_all x1, starting transfers between devices, body(): lax.all_to_all(chosen_spots, 'expert', split_axis=0, concat_axis=2, tiled...  5.1 us
    all_to_all x1, waiting for transfers between devices, body(): lax.all_to_all(lax.all_to_all(chosen_spots, 'expert', split_axis=0, conca...  4.47 us
    gather x1, local copies, waits for them, and re-layouts, body(): trained.reshape(local_experts, block_rows, BLK, block_cols, BLK)  4.04 us
  transfers between devices with their start and end apart: 4, of which 3 were waited for; matrix products, arithmetic and copies ran while one was open for 16% of the time, Pallas kernels for 0%

profile of v1, /device:TPU:1, one launch (start us, length us, event | category | flops | bytes accessed | tf_op | source)
XLA Modules:
  0.0 126.7 jit_solution(16195161585949996241)
XLA Ops:
  0.0 0.9 iota_select_fusion
  2.2 6.4 %all-to-all-start = ((s32[8,4,2]{0,1,2:T(4,128)}), s32[8,4,2]{0,1,2:T(4,128)S(1)}, u32[]{:S(2)}, u32[]{:S(2)}) async-start(s32[8,4,2]{0,1,2:T(4,128)} %broadcast_in_dim.55), calls=%async_computation | async-start | bytes 8192 | tf_op jit(solution)/shard_map/all_to_all | solution.py:59
  9.9 0.8 copy.38
  11.8 0.8 gather_fusion.2
  12.6 4.0 %gather_fusion.1 = f32[32,128,128]{2,1,0:T(8,128)} fusion(f32[8,7,128,1,128]{4,2,1,0,3:T(8,128)} %bitcast.67, s32[32]{0:T(128)S(1)} %reshape.261), kind=kCustom, calls=%fused_computation.1 | custom fusion | bytes 4194688 | tf_op jit(solution)/shard_map/gather | solution.py:43
  16.6 1.9 %convert_subtract_fusion = f32[32,128,128]{2,1,0:T(8,128)S(1)} fusion(f32[32,128,128]{2,1,0:T(8,128)} %gather_fusion.1, bf16[32,128,128]{2,1,0:T(8,128)(2,1)S(1)} %gather_fusion.2), kind=kLoop, calls=%fused_computation.6 | loop fusion | flops 1048576 | bytes 5242880 | tf_op jit(solution)/shard_map/sub | solution.py:50
  18.5 2.3 %fusion.2 = bf16[8,4,128,128]{2,3,1,0:T(8,128)(2,1)S(1)} fusion(f32[8,4,128,128]{3,2,1,0:T(8,128)S(1)} %bitcast.62, pred[8,4]{1,0:T(8,128)(4,1)S(1)} %copy.48, s32[128]{0:T(128)S(1)} %get-tuple-element.7, s32[128]{0:T(128)S(1)} %get-tuple-element.8, s32[128]{0:T(128)S(1)} %get-tuple-element.9, s32[128]{0:T(128)S(1)} %get-tuple-element.10, ...), kind=kOutput, calls=%fused_computation.10 | convolution fusion | flops 806813696 | bytes 3149344 | tf_op jit(solution)/shard_map/ij,pmjk->pmik/dot_general | solution.py:52
  20.8 1.1 copy.49
  21.9 3.6 %all-to-all-start.3 = ((bf16[8,4,2,64,128]{4,3,1,0,2:T(8,128)(2,1)}), bf16[8,4,2,64,128]{4,3,1,0,2:T(8,128)(2,1)S(1)}, u32[]{:S(2)}, u32[]{:S(2)}) async-start(bf16[8,4,2,64,128]{4,3,1,0,2:T(8,128)(2,1)} %copy.49), calls=%async_computation.3 | async-start | bytes 2097152 | tf_op jit(solution)/shard_map/all_to_all | solution.py:58
  27.2 5.1 %all-to-all-start.1 = ((s32[16,1,1,4]{3,2,1,0:T(1,128)}), s32[16,1,1,4]{3,2,1,0:T(1,128)}, u32[]{:S(2)}, u32[]{:S(2)}) async-start(s32[16,1,1,4]{3,2,1,0:T(1,128)} %copy.43), calls=%async_computation.1 | async-start | bytes 16384 | tf_op jit(solution)/shard_map/all_to_all | solution.py:74
  32.3 2.0 %gather_fusion.3 = bf16[16,4,64,128]{3,2,1,0:T(8,128)(2,1)S(1)} fusion(bf16[16,4,64,128]{3,2,1,0:T(8,128)(2,1)} %bitcast.65, s32[1024]{0:T(1024)S(1)} %pad_clamp_fusion), kind=kCustom, calls=%fused_computation.3 | custom fusion | bytes 2097216 | tf_op jit(solution)/shard_map/jit(_take)/gather | solution.py:61
  34.3 1.1 fusion.5
  35.4 3.4 %all-to-all-done.1 = s32[16,1,1,4]{3,2,1,0:T(1,128)} async-done(((s32[16,1,1,4]{3,2,1,0:T(1,128)}), s32[16,1,1,4]{3,2,1,0:T(1,128)}, u32[]{:S(2)}, u32[]{:S(2)}) %all-to-all-start.1) | async-done | bytes 288 | tf_op jit(solution)/shard_map/all_to_all | solution.py:74
  38.8 18.3 %all_to_all.83 = bf16[16,1,1,4,64,128]{5,4,3,2,1,0:T(8,128)(2,1)S(1)} all-to-all(bf16[16,1,1,4,64,128]{5,4,3,2,1,0:T(8,128)(2,1)} %fusion.5), channel_id=1, replica_groups=mesh['expert'=16,'tensor'=8,'replica'=2] {'expert'}, dimensions={0} | all-to-all | bytes 2097152 | tf_op jit(solution)/shard_map/all_to_all | solution.py:67
  57.1 32.4 %all_to_all.84 = bf16[1,1,16,4,64,128]{5,4,3,1,0,2:T(8,128)(2,1)} all-to-all(bf16[1,1,16,4,64,128]{5,4,3,1,0,2:T(8,128)(2,1)S(1)} %bitcast.66), channel_id=1, replica_groups=mesh['expert'=16,'tensor'=8,'replica'=2] {'tensor'}, dimensions={2} | all-to-all | bytes 2097152 | tf_op jit(solution)/shard_map/all_to_all | solution.py:66
  89.6 3.7 %all-to-all-start.2 = ((s32[1,1,16,4]{3,1,0,2:T(1,128)}), s32[1,1,16,4]{3,1,0,2:T(1,128)S(1)}, u32[]{:S(2)}, u32[]{:S(2)}) async-start(s32[1,1,16,4]{3,1,0,2:T(1,128)} %bitcast.31), calls=%async_computation.2 | async-start | bytes 16384 | tf_op jit(solution)/shard_map/all_to_all | solution.py:73
  93.3 2.1 %copy.52 = bf16[1,1,16,4,64,128]{5,3,4,2,1,0:T(4,128)(2,1)S(1)} copy(bf16[1,1,16,4,64,128]{5,4,3,1,0,2:T(8,128)(2,1)} %all_to_all.84) | data formatting | bytes 2097152 | tf_op jit(solution)/shard_map/all_to_all | solution.py:66
  95.4 4.5 %all-to-all-done.2 = s32[1,1,16,4]{3,1,0,2:T(1,128)S(1)} async-done(((s32[1,1,16,4]{3,1,0,2:T(1,128)}), s32[1,1,16,4]{3,1,0,2:T(1,128)S(1)}, u32[]{:S(2)}, u32[]{:S(2)}) %all-to-all-start.2) | async-done | bytes 288 | tf_op jit(solution)/shard_map/all_to_all | solution.py:73
  99.8 1.3 %convert_bitcast_fusion = bf16[1,8,7,64,2,1,128]{6,2,3,4,1,5,0:T(8,128)(2,1)S(1)} fusion(bf16[8,2,4,64,128]{4,2,3,1,0:T(4,128)(2,1)S(1)} %bitcast.64, s32[8,2,4]{2,1,0:T(2,128)S(1)} %bitcast.69), kind=kOutput, calls=%fused_computation.7 | convolution fusion | flops 8257984 | bytes 2883840 | tf_op jit(solution)/shard_map/osnmg,osnmab->osngab/dot_general | solution.py:83
  101.2 3.3 %copy.53 = bf16[1,8,7,64,2,1,128]{6,4,3,2,1,5,0:T(2,128)(2,1)} copy(bf16[1,8,7,64,2,1,128]{6,2,3,4,1,5,0:T(8,128)(2,1)S(1)} %convert_bitcast_fusion) | data formatting | bytes 3670016 | tf_op jit(solution)/shard_map/transpose | solution.py:89
  104.4 5.3 %reshape.227 = bf16[1,8,7,1,64,256]{5,4,2,1,3,0:T(8,128)(2,1)} reshape(bf16[1,8,7,64,2,1,128]{6,4,3,2,1,5,0:T(2,128)(2,1)} %copy.53) | data formatting | bytes 3670016 | tf_op jit(solution)/shard_map/reshape | solution.py:91
  109.7 2.4 %maximum_bitcast_fusion = bf16[1,8,7,2,64,256]{5,4,2,1,0,3:T(8,128)(2,1)S(1)} fusion(bf16[1,8,7,1,64,256]{5,4,2,1,3,0:T(8,128)(2,1)} %reshape.227), kind=kLoop, calls=%fused_computation.5 | loop fusion | flops 1835008 | bytes 5505024 | tf_op jit(solution)/shard_map/concatenate | solution.py:95
  112.1 12.4 %all_to_all.85 = bf16[1,8,7,2,64,256]{5,4,2,1,0,3:T(8,128)(2,1)S(1)} all-to-all(bf16[1,8,7,2,64,256]{5,4,2,1,0,3:T(8,128)(2,1)S(1)} %maximum_bitcast_fusion), channel_id=1, replica_groups=mesh['expert'=16,'tensor'=8,'replica'=2] {'replica'}, dimensions={3} | all-to-all | bytes 7340032 | tf_op jit(solution)/shard_map/all_to_all | solution.py:96
  124.5 2.3 %copy.55 = bf16[1,8,7,2,64,256]{5,4,3,2,1,0:T(8,128)(2,1)} copy(bf16[1,8,7,2,64,256]{5,4,2,1,0,3:T(8,128)(2,1)S(1)} %all_to_all.85) | data formatting | bytes 7340032 | tf_op jit(solution)/shard_map/all_to_all | solution.py:96
  (31 shorter events, 5.5 us)
Async XLA Ops:
  0.0 11.8 %copy-start = (bf16[8,896,128]{2,1,0:T(8,128)(2,1)S(1)}, bf16[8,896,128]{2,1,0:T(8,128)(2,1)}, u32[]{:S(2)}) copy-start(bf16[8,896,128]{2,1,0:T(8,128)(2,1)} %param.5) | copy-start | bytes 5505028
  2.2 19.7 %all-to-all-start = ((s32[8,4,2]{0,1,2:T(4,128)}), s32[8,4,2]{0,1,2:T(4,128)S(1)}, u32[]{:S(2)}, u32[]{:S(2)}) async-start(s32[8,4,2]{0,1,2:T(4,128)} %broadcast_in_dim.55), calls=%async_computation | async-start | bytes 8192 | tf_op jit(solution)/shard_map/all_to_all | solution.py:59
  21.9 5.3 %all-to-all-start.3 = ((bf16[8,4,2,64,128]{4,3,1,0,2:T(8,128)(2,1)}), bf16[8,4,2,64,128]{4,3,1,0,2:T(8,128)(2,1)S(1)}, u32[]{:S(2)}, u32[]{:S(2)}) async-start(bf16[8,4,2,64,128]{4,3,1,0,2:T(8,128)(2,1)} %copy.49), calls=%async_computation.3 | async-start | bytes 2097152 | tf_op jit(solution)/shard_map/all_to_all | solution.py:58
  27.2 5.1 %copy-start.1 = (bf16[8,4,2,64,128]{4,3,1,0,2:T(8,128)(2,1)}, bf16[8,4,2,64,128]{4,3,1,0,2:T(8,128)(2,1)S(1)}, u32[]{:S(2)}) copy-start(bf16[8,4,2,64,128]{4,3,1,0,2:T(8,128)(2,1)S(1)} %all-to-all-done.3) | copy-start | bytes 3145732
  27.2 11.6 %all-to-all-start.1 = ((s32[16,1,1,4]{3,2,1,0:T(1,128)}), s32[16,1,1,4]{3,2,1,0:T(1,128)}, u32[]{:S(2)}, u32[]{:S(2)}) async-start(s32[16,1,1,4]{3,2,1,0:T(1,128)} %copy.43), calls=%async_computation.1 | async-start | bytes 16384 | tf_op jit(solution)/shard_map/all_to_all | solution.py:74
  89.6 10.3 %all-to-all-start.2 = ((s32[1,1,16,4]{3,1,0,2:T(1,128)}), s32[1,1,16,4]{3,1,0,2:T(1,128)S(1)}, u32[]{:S(2)}, u32[]{:S(2)}) async-start(s32[1,1,16,4]{3,1,0,2:T(1,128)} %bitcast.31), calls=%async_computation.2 | async-start | bytes 16384 | tf_op jit(solution)/shard_map/all_to_all | solution.py:73
